TPU v7x, 32 devices: a whole 2x2x4 slice. The times are simulated.
32 devices in a mesh: chain: 16 (over z, x, core), tok: 2 (over y).
Axes of the slice: x: 2, y: 2, z: 4, core: 2. Of those that a mesh axis runs over, the one named last changes fastest.
Arguments:
- queries: bfloat16 [65536, 128], P(('chain', 'tok')), may hold values from -6 to 6
- keys: bfloat16 [65536, 128], P(('chain', 'tok')), may hold values from -6 to 6
- values: bfloat16 [65536, 128], P(('chain', 'tok')), may hold values from -6 to 6
Outputs:
- attended: bfloat16 [65536, 128], P(('chain', 'tok'))
All inputs are finite; a program needn't handle non-finite values.
Results may differ from a plain program's by a relative error of at most 0.0058.
Values may be sent and summed in bfloat16 or wider, within the bound.
A program may use at most 64 MiB of HBM per device.

v0:
```python
import math

import jax
import jax.numpy as jnp
import numpy as np
from jax import lax
from jax.sharding import PartitionSpec as P

HD = 64
HEADS = 2
F = 2080


def entering(part, axis, combine, identity):
    place = lax.axis_index(axis)
    gathered = lax.all_gather(part, axis)
    state = jnp.zeros_like(part) + jnp.asarray(identity, part.dtype)

    def one(step, state):
        return combine(state, lax.dynamic_index_in_dim(gathered, step, 0, False))

    return lax.fori_loop(0, place, one, state)


def tables(width):
    first, second = np.triu_indices(width)
    places = np.arange(width)[:, None]
    first_pick = jnp.asarray((places == first[None, :]).astype(np.float32), jnp.bfloat16)
    second_pick = jnp.asarray((places == second[None, :]).astype(np.float32), jnp.bfloat16)
    scaling = jnp.asarray(np.where(first < second, math.sqrt(2.0), 1.0).astype(np.float32))
    return (first_pick, second_pick, scaling)


def expand(vectors, first_pick, second_pick, scaling):
    left = jnp.einsum("thd,df->hft", vectors, first_pick, preferred_element_type=jnp.bfloat16)
    right = jnp.einsum("thd,df->hft", vectors, second_pick, preferred_element_type=jnp.bfloat16)
    product = left.astype(jnp.float32) * right.astype(jnp.float32) * scaling[None, :, None]
    return product.astype(jnp.bfloat16)


def read_state(query_heads, piece, tables_all):
    first_pick, second_pick, scaling = tables_all
    count = piece.shape[1]
    first_part = lax.slice_in_dim(first_pick, 0, count, axis=1)
    second_part = lax.slice_in_dim(second_pick, 0, count, axis=1)
    scale_part = lax.slice_in_dim(scaling, 0, count, axis=0)
    feats = expand(query_heads, first_part, second_part, scale_part)
    state = piece[0].reshape(count, 2, HD)
    part = jnp.einsum("hft,fhd->thd", feats, state, preferred_element_type=jnp.float32)
    pieces = part.reshape(query_heads.shape[0], 2 * HD)
    return pieces


def add_states(earlier, later):
    return earlier + later


def on_device(queries, keys, values):
    tables_all = tables(HD)
    first_pick, second_pick, scaling = tables_all
    length = queries.shape[0]
    query_heads = queries.reshape(length, HEADS, HD)
    key_heads = keys.reshape(length, HEADS, HD)
    value_heads = values.reshape(length, HEADS, HD)
    feats = expand(key_heads, first_pick, second_pick, scaling)
    state = jnp.einsum("hft,thd->fhd", feats, value_heads, preferred_element_type=jnp.float32)
    states = [state.reshape(F, 2 * HD)]
    local = jnp.stack(states)
    share = lax.psum_scatter(local, "tok", scatter_dimension=1, tiled=True)
    before = entering(share, "chain", add_states, jnp.zeros_like(share))
    inclusive = (before + share).astype(jnp.bfloat16)
    gathered = read_state(
        query_heads, lax.all_gather(inclusive, "tok", axis=1, tiled=True), tables_all
    )
    count = (lax.axis_index("chain") + 1).astype(jnp.float32) * (length * lax.axis_size("tok"))
    return (gathered / (HD * jnp.sqrt(count))).astype(jnp.bfloat16)


def solution(mesh):
    placed = (P(("chain", "tok"), None), P(("chain", "tok"), None), P(("chain", "tok"), None))
    return jax.shard_map(
        on_device, mesh=mesh, in_specs=placed, out_specs=P(("chain", "tok"), None), check_vma=False
    )
```

profile of v0, /device:TPU:27, one launch (start us, length us, event | category | flops | bytes accessed | tf_op | source)
XLA Modules:
  0.0 176.4 jit_solution(14563885322677225598)
XLA Ops:
  6.5 0.0 copy-start.4
  6.5 0.0 copy-start.3
  6.5 0.0 reduce-scatter.2.cloned.1.call-start
  6.5 1.3 copy.19
  7.8 1.2 copy.20
  9.1 9.2 %fusion.18 = bf16[2080,2048,2]{1,0,2:T(8,128)(2,1)} fusion(bf16[64,2080,1]{1,0,2:T(8,128)(2,1)} %constant.33, bf16[2048,2,64]{0,2,1:T(8,128)(2,1)S(1)} %bitcast.41), kind=kOutput, calls=%fused_computation.14 | convolution fusion | flops 1090519040 | bytes 17829888 | tf_op jit(solution)/shard_map/thd,df->hft/dot_general | solution.py:35
  18.3 0.0 copy-done.4
  18.3 0.0 copy-done.3
  18.3 0.0 copy-start.2
  18.3 0.0 copy-start.1
  18.3 13.4 %fusion.1 = f32[2,2080,64]{1,2,0:T(8,128)S(1)} fusion(bf16[2048,2,64]{0,2,1:T(8,128)(2,1)S(1)} %bitcast.47, bf16[2080,2048,2]{1,0,2:T(8,128)(2,1)} %fusion.18, f32[2080]{0:T(1024)S(1)} %copy-done.4, bf16[64,2080,1]{1,0,2:T(8,128)(2,1)S(1)} %copy-done.3, bf16[2048,2,64]{0,2,1:T(8,128)(2,1)S(1)} %bitcast.42), kind=kOutput, calls=%fused_computation.4 | convolution fusion | flops 2223636480 | bytes 19427456 | tf_op jit(solution)/shard_map/hft,thd->fhd/dot_general | solution.py:66
  31.7 1.3 copy.21
  33.1 0.0 reduce-scatter.2.cloned.1.call-update
  33.1 0.0 all-gather.3.cloned.1.call-start
  33.1 21.5 %reduce-scatter.2.cloned.1.call-done = f32[1,1040,128]{2,1,0:T(8,128)} async-done(((f32[1,2080,128]{2,1,0:T(8,128)}), f32[1,1040,128]{2,1,0:T(8,128)}) %reduce-scatter.2.cloned.1.call-update) | async-done | bytes 532496 | tf_op jit(solution)/shard_map/reduce_scatter | solution.py:69
  54.6 0.0 copy-start
  54.6 0.0 all-gather.3.cloned.1.call-update
  54.6 0.0 copy-done.2
  54.7 0.2 copy.24
  54.9 0.0 copy-done.1
  55.0 8.2 %fusion.19 = bf16[2080,2048,2]{1,0,2:T(8,128)(2,1)} fusion(bf16[64,2080,1]{1,0,2:T(8,128)(2,1)S(1)} %copy-done.1, bf16[2048,2,64]{0,2,1:T(8,128)(2,1)S(1)} %bitcast.39), kind=kOutput, calls=%fused_computation.15 | convolution fusion | flops 1090519040 | bytes 17829888 | tf_op jit(solution)/shard_map/thd,df->hft/dot_general | solution.py:35
  63.2 67.1 %all-gather.3.cloned.1.call-done = f32[16,1040,128]{2,1,0:T(8,128)} async-done(((f32[1,1040,128]{2,1,0:T(8,128)}), f32[16,1040,128]{2,1,0:T(8,128)}) %all-gather.3.cloned.1.call-update) | async-done | bytes 8519696 | tf_op jit(solution)/shard_map/all_gather | solution.py:16
  130.3 17.9 %while.10 = (s32[]{:T(128)}, f32[1,1040,128]{2,1,0:T(8,128)S(1)}, s32[]{:T(128)}, f32[16,1,1040,128]{3,2,1,0:T(8,128)}, s32[]{:T(128)}, /*index=5*/s32[]{:T(128)}, s32[]{:T(128)}) while((s32[]{:T(128)}, f32[1,1040,128]{2,1,0:T(8,128)S(1)}, s32[]{:T(128)}, f32[16,1,1040,128]{3,2,1,0:T(8,128)}, s32[]{:T(128)}, /*index=5*/s32[]{:T(128)}, ...), condition=%wide.region_2.3_spmd, body=%wide.region_1.2_spmd.sunk | while | flops 133125 | bytes 1597555 | solution.py:22
  130.3 1.2 bitcast_add_fusion.2
  131.5 1.2 bitcast_add_fusion.2
  132.7 1.2 bitcast_add_fusion.2
  133.9 1.2 bitcast_add_fusion.2
  135.1 1.2 bitcast_add_fusion.2
  136.3 1.2 bitcast_add_fusion.2
  137.5 1.2 bitcast_add_fusion.2
  138.7 1.2 bitcast_add_fusion.2
  139.9 1.2 bitcast_add_fusion.2
  141.1 1.2 bitcast_add_fusion.2
  142.2 1.2 bitcast_add_fusion.2
  143.4 1.2 bitcast_add_fusion.2
  144.6 1.2 bitcast_add_fusion.2
  145.8 1.2 bitcast_add_fusion.2
  147.0 1.2 bitcast_add_fusion.2
  148.2 0.0 copy-done
  148.2 0.1 add_convert_fusion
  148.3 8.5 %all_gather.11 = bf16[1,2080,128]{2,1,0:T(8,128)(2,1)S(1)} all-gather(bf16[1,1040,128]{2,1,0:T(8,128)(2,1)S(1)} %add_convert_fusion), channel_id=1, replica_groups=mesh['chain'=16,'tok'=2] {'tok'}, dimensions={1}, use_global_device_ids=true | all-gather | bytes 798720 | tf_op jit(solution)/shard_map/all_gather | solution.py:73
  156.8 0.3 copy.23
  157.1 11.4 %fusion.15 = bf16[2,64,2048]{2,1,0:T(8,128)(2,1)S(1)} fusion(bf16[2080,2,64]{0,2,1:T(8,128)(2,1)S(1)} %bitcast.45, bf16[2080,2048,2]{1,0,2:T(8,128)(2,1)} %fusion.19, f32[2080]{0:T(1024)S(1)} %copy-done.4, bf16[64,2080,1]{1,0,2:T(8,128)(2,1)S(1)} %copy-done.3, bf16[2048,2,64]{0,2,1:T(8,128)(2,1)S(1)} %bitcast.40, f32[]{:T(128)S(6)} %mul_shard_map.3), kind=kOutput, calls=%fused_computation.12 | convolution fusion | flops 2224160768 | bytes 18894980 | tf_op jit(solution)/shard_map/hft,fhd->thd/dot_general | solution.py:49
  168.5 1.0 copy.25
  (1 shorter events, 0.0 us)
Async XLA Ops:
  6.5 11.8 %copy-start.4 = (f32[2080]{0:T(1024)S(1)}, f32[2080]{0:T(1024)}, u32[]{:S(2)}) copy-start(f32[2080]{0:T(1024)} %constant.32.clone) | copy-start | bytes 24964
  6.5 11.8 %copy-start.3 = (bf16[64,2080,1]{1,0,2:T(8,128)(2,1)S(1)}, bf16[64,2080,1]{1,0,2:T(8,128)(2,1)}, u32[]{:S(2)}) copy-start(bf16[64,2080,1]{1,0,2:T(8,128)(2,1)} %constant.34) | copy-start | bytes 798724
  6.5 48.1 %reduce-scatter.2.cloned.1.call-start = ((), (), s32[]{:S(2)}) async-start(), calls=%async_computation.1 | async-start | bytes 1597440 | tf_op jit(solution)/shard_map/reduce_scatter | solution.py:69
  18.3 36.3 %copy-start.2 = (bf16[2048,128]{1,0:T(8,128)(2,1)S(1)}, bf16[2048,128]{1,0:T(8,128)(2,1)}, u32[]{:S(2)}) copy-start(bf16[2048,128]{1,0:T(8,128)(2,1)} %param.8) | copy-start | bytes 1572868
  18.3 36.6 %copy-start.1 = (bf16[64,2080,1]{1,0,2:T(8,128)(2,1)S(1)}, bf16[64,2080,1]{1,0,2:T(8,128)(2,1)}, u32[]{:S(2)}) copy-start(bf16[64,2080,1]{1,0,2:T(8,128)(2,1)} %constant.33) | copy-start | bytes 798724
  33.1 97.2 %all-gather.3.cloned.1.call-start = ((), (), s32[]{:S(2)}) async-start(), calls=%async_computation.2 | async-start | bytes 9052160 | tf_op jit(solution)/shard_map/all_gather | solution.py:16
  54.6 93.6 %copy-start = (f32[1,1040,128]{2,1,0:T(8,128)S(1)}, f32[1,1040,128]{2,1,0:T(8,128)}, u32[]{:S(2)}) copy-start(f32[1,1040,128]{2,1,0:T(8,128)} %reduce-scatter.2.cloned.1.call-done) | copy-start | bytes 1597444
Sparse Core Ops, SparseCore 0:
  33.2 21.3 reduce-scatter.1
  56.9 73.3 all-gather.2
where the time goes:
time: 177 us; the launch traced here: 176 us
  waiting for transfers between devices  88.6 us (50%)
  matrix products  42.3 us (24%)
  other arithmetic  17.5 us (10%)
  between operations  13.5 us (8%)
  blocking collectives  8.5 us (5%)
  local copies, waits for them, and re-layouts  5.44 us (3%)
    all_gather x1, waiting for transfers between devices, entering(): gathered = lax.all_gather(part, axis)  67.1 us
    reduce_scatter x1, waiting for transfers between devices, on_device(): share = lax.psum_scatter(local, 'tok', scatter_dimension=1, tiled=True)  21.5 us
    dot_general x2, matrix products, expand(): jnp.einsum('thd,df->hft', vectors, first_pick, preferred_element_type=jnp...  17.5 us
    add x15, other arithmetic, add_states(): return earlier + later  17.4 us
    dot_general x1, matrix products, on_device(): jnp.einsum('hft,thd->fhd', feats, value_heads, preferred_element_type=jnp...  13.4 us
    dot_general x1, matrix products, read_state(): jnp.einsum('hft,fhd->thd', feats, state, preferred_element_type=jnp.float32)  11.4 us
    all_gather x1, blocking collectives, on_device(): lax.all_gather(inclusive, 'tok', axis=1, tiled=True)  8.5 us
  transfers between devices with their start and end apart: 2, of which 2 were waited for; matrix products, arithmetic and copies ran while one was open for 5% of the time, Pallas kernels for 0%

commit v1 on v0

v1 whole, which is shorter than its diff:
```python
import functools
import math

import jax
import jax.numpy as jnp
from jax import lax
from jax.experimental import pallas as pl
from jax.experimental.pallas import tpu as pltpu
from jax.sharding import PartitionSpec as P

HD = 64
HEADS = 2
WIDE = HEADS * HD
FAR = HD // 2 + 1
BLOCKS = HD // 4 + 1
MESH = pl.DeviceIdType.MESH
F32, BF16 = jnp.float32, jnp.bfloat16


def layout(n_chain, n_tok):
    inner = 1 << ((n_chain.bit_length() - 1) // 2)
    plane = inner * n_tok
    row_parts = min(8, plane)
    blk_parts = plane // row_parts
    units = -(-BLOCKS // blk_parts)
    count = min(3, units)
    cuts = [-(-units * c // count) for c in range(count + 1)]
    return inner, plane, row_parts, blk_parts, units, cuts


def pairs(low, high):
    return [tuple(range(b, min(b + 2, high))) for b in range(low, high, 2)]


def kernel(n_chain, n_tok, q_ref, k_ref, v_ref, o_ref, xx, zz, vt, qf, acc, tot, got, plane_sum,
           far_got, inc_send, inc, out_t, rs_send, rs_recv, z_send, z_recv, ag_send, ag_recv):
    inner, plane, row_parts, blk_parts, units, cuts = layout(n_chain, n_tok)
    outer = n_chain // inner
    rows = WIDE // row_parts
    tokens = q_ref.shape[0]
    tile = 256 if tokens % 256 == 0 else tokens
    tiles = tokens // tile
    chain, tok = lax.axis_index("chain"), lax.axis_index("tok")
    z, me = chain // inner, (chain % inner) * n_tok + tok
    lane = lax.broadcasted_iota(jnp.int32, (tile, WIDE), 1)
    left = lane < HD

    def in_plane(k):
        peer = (me + k) % plane
        return peer, (z * inner + peer // n_tok, peer % n_tok)

    def along(k):
        return (((z + k) % outer) * inner + chain % inner, tok)

    barrier = pltpu.get_barrier_semaphore()
    for k in range(1, plane):
        pl.semaphore_signal(barrier, inc=1, device_id=in_plane(k)[1], device_id_type=MESH)
    for k in range(1, outer):
        pl.semaphore_signal(barrier, inc=1, device_id=along(k), device_id_type=MESH)

    def prepare(ref):
        @pl.loop(0, tiles)
        def _(t):
            at = pl.ds(pl.multiple_of(t * tile, tile), tile)
            x = ref[at, :].astype(F32)
            other = pltpu.roll(x, HD, 1)
            for h in range(HEADS):
                both = jnp.where(left, x, other) if h == 0 else jnp.where(left, other, x)
                xx[h, at, :] = both
                zz[h, at, :] = jnp.where(left, both, pltpu.roll(both, FAR, 1))

    root2 = math.sqrt(2.0)

    def feats(h, b, at):
        x = xx[h, at, :]
        product = zz[h, at, :] * (x if b == 0 else pltpu.roll(x, b, 1))
        if b == 0:
            scale = jnp.where(left, 1.0, 0.0).astype(F32)
        elif b == 1:
            scale = jnp.where(left, root2, 1.0).astype(F32)
        else:
            scale = jnp.float32(root2)
        return (product * scale).astype(BF16)

    def joined(parts, axis=1):
        return parts[0] if len(parts) == 1 else jnp.concatenate(parts, axis=axis)

    def blocks_of(c):
        return cuts[c] * blk_parts, cuts[c + 1] * blk_parts

    def state(c):
        low, high = blocks_of(c)
        real = min(high, BLOCKS)
        acc[pl.ds(low, high - low)] = jnp.zeros((high - low, WIDE, WIDE), F32)

        @pl.loop(0, tiles)
        def _(t):
            at = pl.ds(pl.multiple_of(t * tile, tile), tile)
            for group in pairs(low, real):
                for h in range(HEADS):
                    part = jnp.dot(vt[pl.ds(h * HD, HD), at],
                                   joined([feats(h, b, at) for b in group]),
                                   preferred_element_type=F32)
                    for i, b in enumerate(group):
                        acc[b, pl.ds(h * HD, HD), :] += part[:, i * WIDE:(i + 1) * WIDE]

        tot[pl.ds(low, high - low)] = acc[pl.ds(low, high - low)].astype(BF16)

    def spot(c, who):
        low, _ = blocks_of(c)
        size = cuts[c + 1] - cuts[c]
        row = pl.multiple_of((who % row_parts) * rows, rows)
        return pl.ds(low + (who // row_parts) * size, size), pl.ds(row, rows)

    def span(c):
        return pl.ds(cuts[c], cuts[c + 1] - cuts[c])

    started = []

    def scatter(c):
        for k in range(1, plane):
            peer, device = in_plane(k)
            blk, row = spot(c, peer)
            copy = pltpu.make_async_remote_copy(
                src_ref=tot.at[blk, row, :], dst_ref=got.at[k, span(c)],
                send_sem=rs_send.at[c, k], recv_sem=rs_recv.at[c, k],
                device_id=device, device_id_type=MESH)
            copy.start()
            started.append(copy)
            rs_copies[c].append(copy)
        blk, row = spot(c, me)
        got[0, span(c)] = tot[blk, row, :]

    def piece(c, source):
        return got[(me + plane - source) % plane, span(c)].astype(F32)

    def spread(c):
        for copy in rs_copies[c]:
            copy.wait_recv()
        total = piece(c, 0)
        for source in range(1, plane):
            total = total + piece(c, source)
        plane_sum[span(c)] = total.astype(BF16)
        for k in range(1, outer):
            copy = pltpu.make_async_remote_copy(
                src_ref=plane_sum.at[span(c)], dst_ref=far_got.at[k, span(c)],
                send_sem=z_send.at[c, k], recv_sem=z_recv.at[c, k],
                device_id=along(k), device_id_type=MESH)
            copy.start()
            started.append(copy)
            z_copies[c].append(copy)

    def gather(c):
        running = jnp.zeros((cuts[c + 1] - cuts[c], rows, WIDE), F32)
        for k in range(1, outer):
            z_copies[c][k - 1].wait_recv()
            running = running + jnp.where(k <= z, far_got[k, span(c)].astype(F32), 0.0)
        for g in range(inner):
            for y in range(n_tok):
                running = running + piece(c, g * n_tok + y)
            inc_send[g, span(c)] = running.astype(BF16)
        blk, row = spot(c, me)
        for k in range(1, plane):
            peer, device = in_plane(k)
            copy = pltpu.make_async_remote_copy(
                src_ref=inc_send.at[peer // n_tok, span(c)], dst_ref=inc.at[blk, row, :],
                send_sem=ag_send.at[c, k], recv_sem=ag_recv.at[c, k],
                device_id=device, device_id_type=MESH)
            copy.start()
            started.append(copy)
            ag_copies[c].append(copy)
        inc[blk, row, :] = inc_send[chain % inner, span(c)]

    def expand_queries(c):
        low, high = blocks_of(c)

        @pl.loop(0, tiles)
        def _(t):
            at = pl.ds(pl.multiple_of(t * tile, tile), tile)
            for b in range(low, min(high, BLOCKS)):
                for h in range(HEADS):
                    qf[h, b, at, :] = feats(h, b, at)

    def read(c, first, last):
        for copy in ag_copies[c]:
            copy.wait_recv()
        low, high = blocks_of(c)
        groups = pairs(low, min(high, BLOCKS))
        count = (chain + 1).astype(F32) * (tokens * n_tok)
        factor = 1.0 / (HD * jnp.sqrt(jnp.full((tile, WIDE), count, F32)))

        @pl.loop(0, tiles)
        def _(t):
            at = pl.ds(pl.multiple_of(t * tile, tile), tile)
            sums = []
            for h in range(HEADS):
                row = pl.ds(h * HD, HD)
                part = None if first else out_t[row, at]
                for group in groups:
                    more = lax.dot_general(
                        joined([inc[b, row, :] for b in group]),
                        joined([qf[h, b, at, :] for b in group]),
                        (((1,), (1,)), ((), ())), preferred_element_type=F32)
                    part = more if part is None else part + more
                if last:
                    sums.append(part)
                else:
                    out_t[row, at] = part
            if last:
                whole = jnp.concatenate(sums, axis=0).T
                o_ref[at, :] = (whole * factor).astype(BF16)

    n = len(cuts) - 1
    rs_copies, z_copies, ag_copies = ([[] for _ in range(n)] for _ in range(3))

    prepare(k_ref)

    @pl.loop(0, tiles)
    def _(t):
        at = pl.ds(pl.multiple_of(t * tile, tile), tile)
        vt[:, at] = v_ref[at, :].astype(F32).T.astype(BF16)

    for c in range(n):
        state(c)
        if c == 0:
            pl.semaphore_wait(barrier, plane - 1 + outer - 1)
        scatter(c)
        if c >= 1:
            spread(c - 1)
    prepare(q_ref)
    for c in range(n):
        expand_queries(c)
        if c == 0:
            spread(n - 1)
        gather(c)
    for c in range(n):
        read(c, c == 0, c == n - 1)
    for copy in started:
        copy.wait_send()


def on_device(n_chain, n_tok, queries, keys, values):
    inner, plane, row_parts, blk_parts, units, cuts = layout(n_chain, n_tok)
    outer, n = n_chain // inner, len(cuts) - 1
    rows, tokens = WIDE // row_parts, queries.shape[0]
    blocks = units * blk_parts
    sems = pltpu.SemaphoreType.DMA
    return pl.pallas_call(
        functools.partial(kernel, n_chain, n_tok),
        out_shape=jax.ShapeDtypeStruct((tokens, WIDE), BF16),
        in_specs=[pl.BlockSpec(memory_space=pltpu.VMEM)] * 3,
        out_specs=pl.BlockSpec(memory_space=pltpu.VMEM),
        scratch_shapes=[
            pltpu.VMEM((HEADS, tokens, WIDE), F32),
            pltpu.VMEM((HEADS, tokens, WIDE), F32),
            pltpu.VMEM((WIDE, tokens), BF16),
            pltpu.VMEM((HEADS, BLOCKS, tokens, WIDE), BF16),
            pltpu.VMEM((blocks, WIDE, WIDE), F32),
            pltpu.VMEM((blocks, WIDE, WIDE), BF16),
            pltpu.VMEM((plane, units, rows, WIDE), BF16),
            pltpu.VMEM((units, rows, WIDE), BF16),
            pltpu.VMEM((max(outer, 1), units, rows, WIDE), BF16),
            pltpu.VMEM((inner, units, rows, WIDE), BF16),
            pltpu.VMEM((blocks, WIDE, WIDE), BF16),
            pltpu.VMEM((WIDE, tokens), F32),
            sems((n, plane)), sems((n, plane)),
            sems((n, max(outer, 1))), sems((n, max(outer, 1))),
            sems((n, plane)), sems((n, plane)),
        ],
        compiler_params=pltpu.CompilerParams(
            collective_id=0, has_side_effects=True, vmem_limit_bytes=60 * 1024 * 1024),
    )(queries, keys, values)


def solution(mesh):
    placed = P(("chain", "tok"), None)
    return jax.shard_map(
        functools.partial(on_device, mesh.shape["chain"], mesh.shape["tok"]),
        mesh=mesh, in_specs=(placed,) * 3, out_specs=placed, check_vma=False)
```

time: 177 us -> 44.7 us (0.25)
  the two profiles are of different devices: /device:TPU:27 before, /device:TPU:1 now
where the time goes in v1:
time: 44.7 us; the launch traced here: 44.5 us
  Pallas kernels  42.7 us (96%)
  local copies, waits for them, and re-layouts  1.87 us (4%)
    pallas_call x1, Pallas kernels, on_device(): pl.pallas_call(functools.partial(kernel, n_chain, n_tok), out_shape=jax.S...  42.7 us
    unnamed x1, local copies, waits for them, and re-layouts  1.87 us

profile of v1, /device:TPU:1, one launch (start us, length us, event | category | flops | bytes accessed | tf_op | source)
XLA Modules:
  0.0 44.5 jit_solution(10929124476003368368)
XLA Ops:
  0.0 42.7 %shard_map.37 = bf16[2048,128]{1,0:T(8,128)(2,1)} custom-call(bf16[2048,128]{1,0:T(8,128)(2,1)} %q_ref.1, bf16[2048,128]{1,0:T(8,128)(2,1)} %k_ref.1, bf16[2048,128]{1,0:T(8,128)(2,1)} %v_ref.1), custom_call_target="tpu_custom_call" | custom-call | tf_op jit(solution)/shard_map/pallas_call | solution.py:248
  42.7 1.9 %copy.5 = bf16[2048,128]{1,0:T(8,128)(2,1)} copy(bf16[2048,128]{1,0:T(8,128)(2,1)} %shard_map.37) | data formatting | bytes 1048576
